TPU v7x, 512 devices: a whole 4x8x8 slice. The times are simulated.
512 devices in a mesh: dp: 32 (over x, y), tensor: 16 (over z, core).
Axes of the slice: x: 4, y: 8, z: 8, core: 2. Of those that a mesh axis runs over, the one named last changes fastest.
Arguments:
- queries: bfloat16 [4096, 16384], P('dp', 'tensor'), may hold values from -24 to 24
- draft_keys: bfloat16 [4096, 1024], P('dp'), may hold values from -6 to 6
- draft_values: bfloat16 [4096, 1024], P('dp'), may hold values from -6 to 6
- cache_keys: bfloat16 [64, 2048, 1024], P('dp', 'tensor'), may hold values from -24 to 24
- cache_values: bfloat16 [64, 2048, 1024], P('dp', 'tensor'), may hold values from -6 to 6
- out_weight: bfloat16 [16384, 16384], P('tensor', 'dp'), may hold values from -0.25 to 0.25
- cache_lengths: int32 [64], P('dp'), may hold values from 512 to 2048
- draft_lengths: int32 [64], replicated, may hold values from 8 to 64
- dest_group: int32 [64], replicated, may hold values from 0 to 31, as said below
- dest_offset: int32 [64], replicated, may hold values from 0 to 32, as said below
Outputs:
- verified: bfloat16 [3072, 16384], P('tensor', 'dp')
Inputs may be any that keep to these rules, and one draw needn't show every extreme that they name: `dest_group`: at most one request of a group has another group as destination, and each group receives at most one such request. `dest_offset`: blocks with the same destination never intersect and end at packed row 96 or before; a block moved to another group starts right after that group's own rows; in every draw some group's blocks fill all 96 rows.
All inputs are finite; a program needn't handle non-finite values.
Results may differ from a plain program's by a relative error of at most 0.017.
Values may be sent and summed in bfloat16 or wider, within the bound.
No kernel may reach another device: no remote copies, remote signals or barrier semaphores. Data moves between devices by JAX's collectives and lax.ppermute only.
A program may use at most 64 MiB of HBM per device.

v0:
```python
import jax
import jax.numpy as jnp
from jax import lax
from jax.sharding import PartitionSpec as P

HEADS = 128
KV_HEADS = 8
HEAD_DIM = 128
DRAFT = 64
GROUP_REQ = 2
PACK = 96
NEG_FILL = -1e30


def packed_sources(row_ids, draft_lengths, dest_group, dest_offset):
    request_ids = jnp.arange(dest_group.shape[0], dtype=jnp.int32)
    slot_group = row_ids // PACK
    slot_index = row_ids % PACK
    inside = (
        (dest_group[None, :] == slot_group[:, None])
        & (slot_index[:, None] >= dest_offset[None, :])
        & (slot_index[:, None] < (dest_offset + draft_lengths)[None, :])
    )
    request = jnp.sum(jnp.where(inside, request_ids[None, :], 0), axis=1)
    first_slot = jnp.sum(jnp.where(inside, dest_offset[None, :], 0), axis=1)
    return (request, slot_index - first_slot, jnp.any(inside, axis=1))


def attend_one(operands):
    queries_one, cache_k, cache_v, draft_k, draft_v, cache_len, draft_len = operands
    score_scale = HEAD_DIM ** (-0.5)
    cache_scores = (
        jnp.einsum("qkgd,lkd->kgql", queries_one, cache_k, preferred_element_type=jnp.float32)
        * score_scale
    )
    draft_scores = (
        jnp.einsum("qkgd,jkd->kgqj", queries_one, draft_k, preferred_element_type=jnp.float32)
        * score_scale
    )
    cache_pos = jnp.arange(cache_k.shape[0], dtype=jnp.int32)
    draft_pos = jnp.arange(draft_k.shape[0], dtype=jnp.int32)
    keep_cache = cache_pos < cache_len
    keep_draft = (draft_pos[None, :] <= draft_pos[:, None]) & (draft_pos[None, :] < draft_len)
    cache_scores = jnp.where(keep_cache, cache_scores, NEG_FILL)
    draft_scores = jnp.where(keep_draft, draft_scores, NEG_FILL)
    highest = jnp.maximum(
        jnp.max(cache_scores, axis=-1, keepdims=True), jnp.max(draft_scores, axis=-1, keepdims=True)
    )
    cache_exp = jnp.exp(cache_scores - highest)
    draft_exp = jnp.exp(draft_scores - highest)
    denominator = jnp.sum(cache_exp, axis=-1, keepdims=True) + jnp.sum(
        draft_exp, axis=-1, keepdims=True
    )
    cache_weights = (cache_exp / denominator).astype(jnp.bfloat16)
    draft_weights = (draft_exp / denominator).astype(jnp.bfloat16)
    mixed = jnp.einsum("kgql,lkd->qkgd", cache_weights, cache_v, preferred_element_type=jnp.float32)
    mixed = mixed + jnp.einsum(
        "kgqj,jkd->qkgd", draft_weights, draft_v, preferred_element_type=jnp.float32
    )
    is_live = draft_pos < draft_len
    return jnp.where(is_live[:, None, None, None], mixed, 0.0).astype(jnp.bfloat16)


def body(
    queries,
    draft_keys,
    draft_values,
    cache_keys,
    cache_values,
    out_weight,
    cache_lengths,
    draft_lengths,
    dest_group,
    dest_offset,
):
    tensor_count = lax.axis_size("tensor")
    data_count = lax.axis_size("dp")
    my_rank = lax.axis_index("tensor")
    my_group = lax.axis_index("dp")
    local_heads = HEADS // tensor_count
    group_heads = HEADS // KV_HEADS
    kv_local = max(1, local_heads // group_heads)
    per_kv = local_heads // kv_local
    kv_width = kv_local * HEAD_DIM
    span_rows = cache_keys.shape[1]
    copies = tensor_count // KV_HEADS

    def spread(cache_block):
        return jnp.repeat(
            cache_block.reshape(GROUP_REQ, span_rows, KV_HEADS, HEAD_DIM), copies, axis=2
        )

    full_keys, full_values = (
        lax.all_to_all(spread(cache_keys), "tensor", split_axis=2, concat_axis=1, tiled=True),
        lax.all_to_all(spread(cache_values), "tensor", split_axis=2, concat_axis=1, tiled=True),
    )
    kv_first = my_rank * local_heads // group_heads
    draft_k = lax.dynamic_slice_in_dim(draft_keys, kv_first * HEAD_DIM, kv_width, 1).reshape(
        GROUP_REQ, DRAFT, kv_local, HEAD_DIM
    )
    draft_v = lax.dynamic_slice_in_dim(draft_values, kv_first * HEAD_DIM, kv_width, 1).reshape(
        GROUP_REQ, DRAFT, kv_local, HEAD_DIM
    )
    local_queries = queries.reshape(GROUP_REQ, DRAFT, kv_local, per_kv, HEAD_DIM)
    my_lengths = lax.dynamic_slice_in_dim(draft_lengths, my_group * GROUP_REQ, GROUP_REQ)
    attended = lax.map(
        attend_one,
        (local_queries, full_keys, full_values, draft_k, draft_v, cache_lengths, my_lengths),
    )
    width_local = local_heads * HEAD_DIM
    attended_rows = attended.reshape(GROUP_REQ * DRAFT, width_local)
    target_rows = PACK * data_count // tensor_count
    home_all = lax.all_gather(attended_rows, "dp", axis=0, tiled=True)
    row_ids = jnp.arange(lax.axis_size("tensor") * target_rows, dtype=jnp.int32)
    request, within, is_live = packed_sources(row_ids, draft_lengths, dest_group, dest_offset)
    picked = jnp.take(home_all, request * DRAFT + within, axis=0)
    picked = jnp.where(is_live[:, None], picked, jnp.zeros((), jnp.bfloat16))
    return lax.psum_scatter(
        jnp.dot(picked, out_weight, preferred_element_type=jnp.float32).astype(jnp.bfloat16),
        "tensor",
        scatter_dimension=0,
        tiled=True,
    )


def solution(mesh):
    in_specs = (
        P("dp", "tensor"),
        P("dp", None),
        P("dp", None),
        P("dp", "tensor", None),
        P("dp", "tensor", None),
        P("tensor", "dp"),
        P("dp"),
        P(),
        P(),
        P(),
    )
    out_specs = P("tensor", "dp")
    return jax.shard_map(body, mesh=mesh, in_specs=in_specs, out_specs=out_specs, check_vma=False)
```

profile of v0, /device:TPU:8, one launch (start us, length us, event | category | flops | bytes accessed | tf_op | source)
XLA Modules:
  0.0 296.0 jit_solution(7023909836648568548)
XLA Ops:
  6.5 1.3 copy_bitcast_fusion.3
  7.9 1.2 broadcast_in_dim.102
  9.1 10.4 %all-to-all-start.1 = ((bf16[2,128,16,128]{3,1,0,2:T(8,128)(2,1)}), bf16[2,128,16,128]{3,1,0,2:T(8,128)(2,1)S(1)}, u32[]{:S(2)}, u32[]{:S(2)}) async-start(bf16[2,128,16,128]{3,1,0,2:T(8,128)(2,1)} %bitcast.25), calls=%async_computation.1 | async-start | bytes 2097152 | tf_op jit(solution)/shard_map/all_to_all | solution.py:94
  19.7 26.3 %all-to-all-done.1 = bf16[2,128,16,128]{3,1,0,2:T(8,128)(2,1)S(1)} async-done(((bf16[2,128,16,128]{3,1,0,2:T(8,128)(2,1)}), bf16[2,128,16,128]{3,1,0,2:T(8,128)(2,1)S(1)}, u32[]{:S(2)}, u32[]{:S(2)}) %all-to-all-start.1) | async-done | bytes 1048608 | tf_op jit(solution)/shard_map/all_to_all | solution.py:94
  46.0 1.3 broadcast_in_dim.101
  47.3 5.0 %all-to-all-start = ((bf16[2,128,16,128]{3,1,0,2:T(8,128)(2,1)}), bf16[2,128,16,128]{3,1,0,2:T(8,128)(2,1)}, u32[]{:S(2)}, u32[]{:S(2)}) async-start(bf16[2,128,16,128]{3,1,0,2:T(8,128)(2,1)} %bitcast.20), calls=%async_computation | async-start | bytes 2097152 | tf_op jit(solution)/shard_map/all_to_all | solution.py:95
  52.5 0.8 constant_dynamic-slice_fusion.1
  53.4 25.4 %all-to-all-done = bf16[2,128,16,128]{3,1,0,2:T(8,128)(2,1)} async-done(((bf16[2,128,16,128]{3,1,0,2:T(8,128)(2,1)}), bf16[2,128,16,128]{3,1,0,2:T(8,128)(2,1)}, u32[]{:S(2)}, u32[]{:S(2)}) %all-to-all-start) | async-done | bytes 1048608 | tf_op jit(solution)/shard_map/all_to_all | solution.py:95
  78.8 1.3 copy.36
  80.1 14.2 %while.10 = (s32[]{:T(128)}, bf16[2,64,1,8,128]{4,3,1,0,2:T(8,128)(2,1)}, s32[2]{0:T(128)S(1)}, bf16[2,2048,1,128]{3,1,2,0:T(8,128)(2,1)S(1)}, s32[2]{0:T(128)S(...) while((s32[]{:T(128)}, ...), condition=%wide.region_8.9_spmd, body=%wide.region_3.8_spmd.sunk | while | flops 566699072 | bytes 15692581 | solution.py:106
  83.2 0.9 bitcast_reduce_fusion.2
  84.2 0.9 fusion.71
  85.1 1.1 fusion.73
  86.5 0.7 copy_dynamic-update-slice_fusion.2
  89.3 0.7 iota_compare_fusion.5
  90.3 0.9 bitcast_reduce_fusion.2
  91.3 0.9 fusion.71
  92.2 1.1 fusion.73
  93.6 0.7 copy_dynamic-update-slice_fusion.2
  94.3 1.7 copy.62
  97.0 99.9 %all-gather.2.cloned.1.call-done = bf16[4096,1024]{1,0:T(8,128)(2,1)} async-done(((bf16[128,1024]{1,0:T(8,128)(2,1)}), bf16[4096,1024]{1,0:T(8,128)(2,1)}) %all-gather.2.cloned.1.call-update) | async-done | bytes 8388624 | tf_op jit(solution)/shard_map/all_gather | solution.py:113
  196.9 20.4 %gather_fusion = bf16[3072,1024]{1,0:T(8,128)(2,1)} fusion(bf16[4096,1024]{1,0:T(8,128)(2,1)} %all-gather.2.cloned.1.call-done, s32[3072]{0:T(1024)S(1)} %broadcast_clamp_fusion), kind=kCustom, calls=%fused_computation | custom fusion | bytes 12595200 | tf_op jit(solution)/shard_map/jit(_take)/gather | solution.py:116
  217.3 7.6 %fusion.34 = bf16[3072,512]{1,0:T(8,128)(2,1)} fusion(bf16[1024,512]{1,0:T(8,128)(2,1)S(1)} %copy-done, bf16[3072,1024]{1,0:T(8,128)(2,1)} %gather_fusion, pred[3072]{0:T(1024)(128)(4,1)S(1)} %compare_and_fusion.1, pred[3072]{0:T(1024)(128)(4,1)S(1)} %fusion.50), kind=kOutput, calls=%fused_computation.49 | convolution fusion | flops 3229089792 | bytes 10491904 | tf_op jit(solution)/shard_map/dot_general | solution.py:119
  224.9 64.2 %reduce-scatter.2.cloned.1.call-done = bf16[192,512]{1,0:T(8,128)(2,1)} async-done(((bf16[3072,512]{1,0:T(8,128)(2,1)}), bf16[192,512]{1,0:T(8,128)(2,1)}) %reduce-scatter.2.cloned.1.call-update) | async-done | bytes 196624 | tf_op jit(solution)/shard_map/reduce_scatter | solution.py:118
  (52 shorter events, 7.4 us)
Async XLA Ops:
  6.5 210.7 %copy-start = (bf16[1024,512]{1,0:T(8,128)(2,1)S(1)}, bf16[1024,512]{1,0:T(8,128)(2,1)}, u32[]{:S(2)}) copy-start(bf16[1024,512]{1,0:T(8,128)(2,1)} %param.17) | copy-start | bytes 3145732
  6.5 13.0 %copy-start.1 = (bf16[2,128,1024]{2,1,0:T(8,128)(2,1)S(1)}, bf16[2,128,1024]{2,1,0:T(8,128)(2,1)}, u32[]{:S(2)}) copy-start(bf16[2,128,1024]{2,1,0:T(8,128)(2,1)} %param.16) | copy-start | bytes 1572868
  7.8 44.5 %copy-start.2 = (bf16[128,1024]{1,0:T(8,128)(2,1)S(1)}, bf16[128,1024]{1,0:T(8,128)(2,1)}, u32[]{:S(2)}) copy-start(bf16[128,1024]{1,0:T(8,128)(2,1)} %param.12) | copy-start | bytes 786436
  7.8 44.6 %copy-start.6 = (s32[64]{0:T(128)S(1)}, s32[64]{0:T(128)}, u32[]{:S(2)}) copy-start(s32[64]{0:T(128)} %param.19) | copy-start | bytes 772
  9.1 36.9 %all-to-all-start.1 = ((bf16[2,128,16,128]{3,1,0,2:T(8,128)(2,1)}), bf16[2,128,16,128]{3,1,0,2:T(8,128)(2,1)S(1)}, u32[]{:S(2)}, u32[]{:S(2)}) async-start(bf16[2,128,16,128]{3,1,0,2:T(8,128)(2,1)} %bitcast.25), calls=%async_computation.1 | async-start | bytes 2097152 | tf_op jit(solution)/shard_map/all_to_all | solution.py:94
  19.7 60.4 %copy-start.5 = (s32[2]{0:T(128)S(1)}, s32[2]{0:T(128)}, u32[]{:S(2)}) copy-start(s32[2]{0:T(128)} %param.18) | copy-start | bytes 28
  47.3 31.5 %all-to-all-start = ((bf16[2,128,16,128]{3,1,0,2:T(8,128)(2,1)}), bf16[2,128,16,128]{3,1,0,2:T(8,128)(2,1)}, u32[]{:S(2)}, u32[]{:S(2)}) async-start(bf16[2,128,16,128]{3,1,0,2:T(8,128)(2,1)} %bitcast.20), calls=%async_computation | async-start | bytes 2097152 | tf_op jit(solution)/shard_map/all_to_all | solution.py:95
  52.3 144.6 %all-gather.2.cloned.1.call-start = ((), (), s32[]{:S(2)}) async-start(), calls=%async_computation.3 | async-start | bytes 8650752 | tf_op jit(solution)/shard_map/all_gather | solution.py:113
  80.1 16.0 %copy-start.3 = (s32[64]{0:T(128)S(1)}, s32[64]{0:T(128)}, u32[]{:S(2)}) copy-start(s32[64]{0:T(128)} %param.21) | copy-start | bytes 772
  80.1 16.0 %copy-start.4 = (s32[64]{0:T(128)S(1)}, s32[64]{0:T(128)}, u32[]{:S(2)}) copy-start(s32[64]{0:T(128)} %param.20) | copy-start | bytes 772
  96.0 193.2 %reduce-scatter.2.cloned.1.call-start = ((), (), s32[]{:S(2)}) async-start(), calls=%async_computation.4 | async-start | bytes 3342336 | tf_op jit(solution)/shard_map/reduce_scatter | solution.py:118
Sparse Core Ops, SparseCore 0:
  96.1 100.6 all-gather.1
  225.1 64.0 reduce-scatter.1
where the time goes:
time: 297 us; the launch traced here: 296 us
  waiting for transfers between devices  216 us (73%)
  local copies, waits for them, and re-layouts  32.5 us (11%)
  starting transfers between devices  15.5 us (5%)
  between operations  13.6 us (5%)
  matrix products  12.5 us (4%)
  other arithmetic  5.82 us (2%)
    all_gather x1, waiting for transfers between devices, body(): home_all = lax.all_gather(attended_rows, 'dp', axis=0, tiled=True)  99.9 us
    reduce_scatter x1, waiting for transfers between devices, body(): lax.psum_scatter(jnp.dot(picked, out_weight, preferred_element_type=jnp.f...  64.2 us
    all_to_all x1, waiting for transfers between devices, body(): lax.all_to_all(spread(cache_keys), 'tensor', split_axis=2, concat_axis=1,...  26.3 us
    all_to_all x1, waiting for transfers between devices, body(): lax.all_to_all(spread(cache_values), 'tensor', split_axis=2, concat_axis=...  25.4 us
    gather x1, local copies, waits for them, and re-layouts, body(): picked = jnp.take(home_all, request * DRAFT + within, axis=0)  20.4 us
    all_to_all x1, starting transfers between devices, body(): lax.all_to_all(spread(cache_keys), 'tensor', split_axis=2, concat_axis=1,...  10.4 us
    dot_general x1, matrix products, body(): jnp.dot(picked, out_weight, preferred_element_type=jnp.float32)  7.65 us
  transfers between devices with their start and end apart: 4, of which 4 were waited for; matrix products, arithmetic and copies ran while one was open for 1% of the time, Pallas kernels for 0%

commit v1 on v0

--- a/solution.py
+++ b/solution.py
@@ -110,7 +110,9 @@
     width_local = local_heads * HEAD_DIM
     attended_rows = attended.reshape(GROUP_REQ * DRAFT, width_local)
     target_rows = PACK * data_count // tensor_count
-    home_all = lax.all_gather(attended_rows, "dp", axis=0, tiled=True)
+    home_all = jnp.concatenate(
+        lax.all_to_all(jnp.stack([attended_rows] * lax.axis_size("dp")), "dp", 0, 0), axis=0
+    )
     row_ids = jnp.arange(lax.axis_size("tensor") * target_rows, dtype=jnp.int32)
     request, within, is_live = packed_sources(row_ids, draft_lengths, dest_group, dest_offset)
     picked = jnp.take(home_all, request * DRAFT + within, axis=0)

time: 297 us -> 408 us (1.37)
  waiting for transfers between devices: 216 us -> 312 us
  starting transfers between devices: 15.5 us -> 25.7 us
  local copies, waits for them, and re-layouts: 32.5 us -> 36.8 us
    all_to_all x0 -> x1, waiting for transfers between devices: none -> 194 us  [body(): lax.all_to_all(jnp.stack([attended_rows] * lax.axis_size('dp')), 'dp', 0, 0)]
    all_gather x1 -> x0, waiting for transfers between devices: 99.9 us -> none  [body(): home_all = lax.all_gather(attended_rows, 'dp', axis=0, tiled=True)]
    all_to_all x0 -> x1, starting transfers between devices: none -> 10.3 us  [body(): lax.all_to_all(jnp.stack([attended_rows] * lax.axis_size('dp')), 'dp', 0, 0)]
    all_to_all x1, starting transfers between devices: 10.4 us -> 4.93 us  [body(): lax.all_to_all(spread(cache_keys), 'tensor', split_axis=2, concat_axis=1,...]
    all_to_all x1, starting transfers between devices: 4.98 us -> 10.4 us  [body(): lax.all_to_all(spread(cache_values), 'tensor', split_axis=2, concat_axis=...]
    another operation x0 -> x1, local copies, waits for them, and re-layouts: none -> 4.28 us  [body(): jnp.stack([attended_rows] * lax.axis_size('dp'))]
    reduce_scatter x1, waiting for transfers between devices: 64.2 us -> 68.4 us  [body(): lax.psum_scatter(jnp.dot(picked, out_weight, preferred_element_type=jnp.f...]
where the time goes in v1:
time: 408 us; the launch traced here: 407 us
  waiting for transfers between devices  312 us (76%)
  local copies, waits for them, and re-layouts  36.8 us (9%)
  starting transfers between devices  25.7 us (6%)
  between operations  13.6 us (3%)
  matrix products  12.5 us (3%)
  other arithmetic  5.83 us (1%)
    all_to_all x1, waiting for transfers between devices, body(): lax.all_to_all(jnp.stack([attended_rows] * lax.axis_size('dp')), 'dp', 0, 0)  194 us
    reduce_scatter x1, waiting for transfers between devices, body(): lax.psum_scatter(jnp.dot(picked, out_weight, preferred_element_type=jnp.f...  68.4 us
    all_to_all x1, waiting for transfers between devices, body(): lax.all_to_all(spread(cache_values), 'tensor', split_axis=2, concat_axis=...  26.3 us
    all_to_all x1, waiting for transfers between devices, body(): lax.all_to_all(spread(cache_keys), 'tensor', split_axis=2, concat_axis=1,...  23.5 us
    gather x1, local copies, waits for them, and re-layouts, body(): picked = jnp.take(home_all, request * DRAFT + within, axis=0)  20.4 us
    all_to_all x1, starting transfers between devices, body(): lax.all_to_all(spread(cache_values), 'tensor', split_axis=2, concat_axis=...  10.4 us
    all_to_all x1, starting transfers between devices, body(): lax.all_to_all(jnp.stack([attended_rows] * lax.axis_size('dp')), 'dp', 0, 0)  10.3 us
  transfers between devices with their start and end apart: 4, of which 4 were waited for; matrix products, arithmetic and copies ran while one was open for 1% of the time, Pallas kernels for 0%

profile of v1, /device:TPU:8, one launch (start us, length us, event | category | flops | bytes accessed | tf_op | source)
XLA Modules:
  0.0 407.1 jit_solution(17798751463874585295)
XLA Ops:
  6.5 1.3 copy_bitcast_fusion.4
  7.8 1.2 broadcast_in_dim.101
  9.1 10.4 %all-to-all-start = ((bf16[2,128,16,128]{3,1,0,2:T(8,128)(2,1)}), bf16[2,128,16,128]{3,1,0,2:T(8,128)(2,1)S(1)}, u32[]{:S(2)}, u32[]{:S(2)}) async-start(bf16[2,128,16,128]{3,1,0,2:T(8,128)(2,1)} %bitcast.20), calls=%async_computation | async-start | bytes 2097152 | tf_op jit(solution)/shard_map/all_to_all | solution.py:95
  19.7 26.3 %all-to-all-done = bf16[2,128,16,128]{3,1,0,2:T(8,128)(2,1)S(1)} async-done(((bf16[2,128,16,128]{3,1,0,2:T(8,128)(2,1)}), bf16[2,128,16,128]{3,1,0,2:T(8,128)(2,1)S(1)}, u32[]{:S(2)}, u32[]{:S(2)}) %all-to-all-start) | async-done | bytes 1048608 | tf_op jit(solution)/shard_map/all_to_all | solution.py:95
  46.0 1.3 broadcast_in_dim.102
  47.3 4.9 %all-to-all-start.1 = ((bf16[2,128,16,128]{3,1,0,2:T(8,128)(2,1)}), bf16[2,128,16,128]{3,1,0,2:T(8,128)(2,1)S(1)}, u32[]{:S(2)}, u32[]{:S(2)}) async-start(bf16[2,128,16,128]{3,1,0,2:T(8,128)(2,1)} %bitcast.163), calls=%async_computation.1 | async-start | bytes 2097152 | tf_op jit(solution)/shard_map/all_to_all | solution.py:94
  52.2 1.0 copy.48
  53.3 0.8 constant_dynamic-slice_fusion.1
  54.1 1.1 copy.35
  55.2 23.5 %all-to-all-done.1 = bf16[2,128,16,128]{3,1,0,2:T(8,128)(2,1)S(1)} async-done(((bf16[2,128,16,128]{3,1,0,2:T(8,128)(2,1)}), bf16[2,128,16,128]{3,1,0,2:T(8,128)(2,1)S(1)}, u32[]{:S(2)}, u32[]{:S(2)}) %all-to-all-start.1) | async-done | bytes 1048608 | tf_op jit(solution)/shard_map/all_to_all | solution.py:94
  78.8 14.2 %while.10 = (s32[]{:T(128)}, bf16[2,64,1,8,128]{4,3,1,0,2:T(8,128)(2,1)}, s32[2]{0:T(128)S(1)}, bf16[2,2048,1,128]{3,1,2,0:T(8,128)(2,1)}, s32[2]{0:T(128)S(1)},...) while((s32[]{:T(128)}, ...), condition=%wide.region_8.9_spmd, body=%wide.region_3.8_spmd.sunk | while | flops 566699072 | bytes 19887412 | solution.py:106
  80.2 0.9 bitcast_reduce_fusion.2
  82.9 1.0 fusion.71
  83.8 1.1 fusion.73
  87.3 0.9 bitcast_reduce_fusion.2
  90.0 1.0 fusion.71
  90.9 1.1 fusion.73
  93.0 1.0 copy.61
  94.0 4.3 %stack.3 = bf16[32,128,1024]{2,1,0:T(8,128)(2,1)} broadcast(bf16[128,1024]{1,0:T(8,128)(2,1)S(1)} %bitcast.165), dimensions={1,2} | broadcast | bytes 8650752 | tf_op jit(solution)/shard_map/stack | solution.py:114
  98.3 10.3 %all-to-all-start.2 = ((bf16[32,128,1024]{2,1,0:T(8,128)(2,1)}), bf16[32,128,1024]{2,1,0:T(8,128)(2,1)}, u32[]{:S(2)}, u32[]{:S(2)}) async-start(bf16[32,128,1024]{2,1,0:T(8,128)(2,1)} %stack.3), calls=%async_computation.2 | async-start | bytes 16777216 | tf_op jit(solution)/shard_map/all_to_all | solution.py:114
  109.6 194.1 %all-to-all-done.2 = bf16[32,128,1024]{2,1,0:T(8,128)(2,1)} async-done(((bf16[32,128,1024]{2,1,0:T(8,128)(2,1)}), bf16[32,128,1024]{2,1,0:T(8,128)(2,1)}, u32[]{:S(2)}, u32[]{:S(2)}) %all-to-all-start.2) | async-done | bytes 8388640 | tf_op jit(solution)/shard_map/all_to_all | solution.py:114
  303.8 20.4 %gather_fusion = bf16[3072,1024]{1,0:T(8,128)(2,1)} fusion(bf16[4096,1024]{1,0:T(8,128)(2,1)} %bitcast.32, s32[3072]{0:T(1024)S(1)} %broadcast_clamp_fusion), kind=kCustom, calls=%fused_computation | custom fusion | bytes 12595200 | tf_op jit(solution)/shard_map/jit(_take)/gather | solution.py:118
  324.2 7.6 %fusion.34 = bf16[3072,512]{1,0:T(8,128)(2,1)} fusion(bf16[1024,512]{1,0:T(8,128)(2,1)S(1)} %copy-done, bf16[3072,1024]{1,0:T(8,128)(2,1)} %gather_fusion, pred[3072]{0:T(1024)(128)(4,1)S(1)} %compare_and_fusion.1, pred[3072]{0:T(1024)(128)(4,1)S(1)} %fusion.50), kind=kOutput, calls=%fused_computation.49 | convolution fusion | flops 3229089792 | bytes 10491904 | tf_op jit(solution)/shard_map/dot_general | solution.py:121
  331.8 68.4 %reduce-scatter.2.cloned.1.call-done = bf16[192,512]{1,0:T(8,128)(2,1)} async-done(((bf16[3072,512]{1,0:T(8,128)(2,1)}), bf16[192,512]{1,0:T(8,128)(2,1)}) %reduce-scatter.2.cloned.1.call-update) | async-done | bytes 196624 | tf_op jit(solution)/shard_map/reduce_scatter | solution.py:120
  (54 shorter events, 9.5 us)
Async XLA Ops:
  6.5 317.6 %copy-start = (bf16[1024,512]{1,0:T(8,128)(2,1)S(1)}, bf16[1024,512]{1,0:T(8,128)(2,1)}, u32[]{:S(2)}) copy-start(bf16[1024,512]{1,0:T(8,128)(2,1)} %param.17) | copy-start | bytes 3145732
  6.5 13.0 %copy-start.2 = (bf16[2,128,1024]{2,1,0:T(8,128)(2,1)S(1)}, bf16[2,128,1024]{2,1,0:T(8,128)(2,1)}, u32[]{:S(2)}) copy-start(bf16[2,128,1024]{2,1,0:T(8,128)(2,1)} %param.15) | copy-start | bytes 1572868
  7.8 45.4 %copy-start.6 = (s32[64]{0:T(128)S(1)}, s32[64]{0:T(128)}, u32[]{:S(2)}) copy-start(s32[64]{0:T(128)} %param.19) | copy-start | bytes 772
  9.1 36.9 %all-to-all-start = ((bf16[2,128,16,128]{3,1,0,2:T(8,128)(2,1)}), bf16[2,128,16,128]{3,1,0,2:T(8,128)(2,1)S(1)}, u32[]{:S(2)}, u32[]{:S(2)}) async-start(bf16[2,128,16,128]{3,1,0,2:T(8,128)(2,1)} %bitcast.20), calls=%async_computation | async-start | bytes 2097152 | tf_op jit(solution)/shard_map/all_to_all | solution.py:95
  19.6 59.2 %copy-start.5 = (s32[2]{0:T(128)S(1)}, s32[2]{0:T(128)}, u32[]{:S(2)}) copy-start(s32[2]{0:T(128)} %param.18) | copy-start | bytes 28
  47.3 31.4 %all-to-all-start.1 = ((bf16[2,128,16,128]{3,1,0,2:T(8,128)(2,1)}), bf16[2,128,16,128]{3,1,0,2:T(8,128)(2,1)S(1)}, u32[]{:S(2)}, u32[]{:S(2)}) async-start(bf16[2,128,16,128]{3,1,0,2:T(8,128)(2,1)} %bitcast.163), calls=%async_computation.1 | async-start | bytes 2097152 | tf_op jit(solution)/shard_map/all_to_all | solution.py:94
  80.2 3.6 copy-start.1
  87.3 3.6 copy-start.1
  98.3 10.4 %copy-start.3 = (s32[64]{0:T(128)S(1)}, s32[64]{0:T(128)}, u32[]{:S(2)}) copy-start(s32[64]{0:T(128)} %param.21) | copy-start | bytes 772
  98.3 10.5 %copy-start.4 = (s32[64]{0:T(128)S(1)}, s32[64]{0:T(128)}, u32[]{:S(2)}) copy-start(s32[64]{0:T(128)} %param.20) | copy-start | bytes 772
  98.3 205.5 %all-to-all-start.2 = ((bf16[32,128,1024]{2,1,0:T(8,128)(2,1)}), bf16[32,128,1024]{2,1,0:T(8,128)(2,1)}, u32[]{:S(2)}, u32[]{:S(2)}) async-start(bf16[32,128,1024]{2,1,0:T(8,128)(2,1)} %stack.3), calls=%async_computation.2 | async-start | bytes 16777216 | tf_op jit(solution)/shard_map/all_to_all | solution.py:114
  108.7 291.6 %reduce-scatter.2.cloned.1.call-start = ((), (), s32[]{:S(2)}) async-start(), calls=%async_computation.4 | async-start | bytes 3342336 | tf_op jit(solution)/shard_map/reduce_scatter | solution.py:120
Sparse Core Ops, SparseCore 0:
  332.0 68.2 reduce-scatter.1
